TPU v7x, 32 devices: a whole 2x2x4 slice. The times are simulated.
32 devices in a mesh: fsdp: 16 (over z, x, core), tp: 2 (over y).
Axes of the slice: x: 2, y: 2, z: 4, core: 2. Of those that a mesh axis runs over, the one named last changes fastest.
Arguments:
- tokens: bfloat16 [2048, 3584], P('fsdp', 'tp'), may hold values from -6 to 6
- norm_gain: bfloat16 [3584], replicated, may hold values from 0.5 to 1.5
- gate_weight: bfloat16 [3584, 10240], P('fsdp', 'tp'), may hold values from -0.09375 to 0.09375
- up_weight: bfloat16 [3584, 10240], P('fsdp', 'tp'), may hold values from -0.09375 to 0.09375
- down_weight: bfloat16 [3584, 10240], P('fsdp', 'tp'), may hold values from -0.0625 to 0.0625
- probes: bfloat16 [2, 3584, 10240], P(None, 'fsdp', 'tp'), may hold values from -0.0625 to 0.0625
Outputs:
- layer_out: bfloat16 [2048, 3584], P('tp', 'fsdp')
- token_curv: float32 [2048], P('tp')
All inputs are finite; a program needn't handle non-finite values.
Results may differ from a plain program's by a relative error of at most 0.014.
Values may be sent and summed in bfloat16 or wider, within the bound.
A program may use at most 128 MiB of HBM per device.

v0:
```python
import jax
import jax.numpy as jnp
from jax import lax
from jax.sharding import PartitionSpec as P

D = 3584
PROBES = 2


epsilon = 1e-06


def on_device(tokens, norm_gain, gate_weight, up_weight, down_weight, probes):
    features = lax.all_gather(tokens, "tp", axis=1, tiled=True)
    widened = features.astype(jnp.float32)
    inverse_rms = lax.rsqrt(jnp.mean(widened * widened, axis=1, keepdims=True) + epsilon)
    normed = (widened * inverse_rms * norm_gain.astype(jnp.float32)).astype(jnp.bfloat16)

    def add_rows(shard_rows):
        return jnp.dot(normed, shard_rows, preferred_element_type=jnp.float32)

    gate_sum = add_rows(lax.all_gather(gate_weight, "fsdp", axis=0, tiled=True))
    up_sum = add_rows(lax.all_gather(up_weight, "fsdp", axis=0, tiled=True))
    hidden = (jax.nn.silu(gate_sum) * up_sum).astype(jnp.bfloat16)
    stacked = jnp.concatenate([down_weight[None], probes], axis=0)
    count = stacked.shape[0]
    col_width = stacked.shape[1]
    flat_weights = stacked.reshape(count * col_width, stacked.shape[2])
    partial_terms = lax.dot_general(
        lax.all_gather(hidden, "fsdp", axis=0, tiled=True),
        flat_weights,
        (((1,), (1,)), ((), ())),
        preferred_element_type=jnp.float32,
    )
    summed = lax.psum_scatter(
        partial_terms.astype(jnp.bfloat16), "tp", scatter_dimension=0, tiled=True
    ).astype(jnp.float32)
    summed_parts = summed.reshape(summed.shape[0], count, col_width)
    primal = summed_parts[:, 0, :]
    tangents = summed_parts[:, 1:, :]
    squashed = jax.nn.sigmoid(primal)
    slope = squashed * (1.0 - squashed)
    tangent_sq = jnp.sum(tangents * tangents, axis=1)
    local_curv = jnp.sum(slope * tangent_sq, axis=1) / (PROBES * D)
    token_curv = lax.psum(local_curv, "fsdp")
    return (primal.astype(jnp.bfloat16), token_curv)


def solution(mesh):
    return jax.shard_map(
        on_device,
        mesh=mesh,
        in_specs=(
            P("fsdp", "tp"),
            P(),
            P("fsdp", "tp"),
            P("fsdp", "tp"),
            P("fsdp", "tp"),
            P(None, "fsdp", "tp"),
        ),
        out_specs=(P("tp", "fsdp"), P("tp")),
        check_vma=False,
    )
```

profile of v0, /device:TPU:0, one launch (start us, length us, event | category | flops | bytes accessed | tf_op | source)
XLA Modules:
  0.0 610.9 jit_solution(12991252066868905236)
XLA Ops:
  7.2 0.0 copy-start.1
  7.2 0.0 copy-start
  7.2 0.0 all-gather.4.cloned.1.call-start
  7.2 0.7 all-gather.4.cloned.1.call-update
  7.9 0.0 all-gather.6.cloned.1.call-start
  8.0 0.7 all-gather.6.cloned.1.call-update
  8.7 0.0 all-gather.8.cloned.1.call-start
  8.7 0.0 copy-done.1
  8.7 0.0 copy-done
  8.7 14.2 %all_gather.12 = bf16[128,3584]{1,0:T(8,128)(2,1)S(1)} all-gather(bf16[128,1792]{1,0:T(8,128)(2,1)S(1)} %copy-done), channel_id=1, replica_groups=mesh['fsdp'=16,'tp'=2] {'tp'}, dimensions={1}, use_global_device_ids=true | all-gather | bytes 1376256 | tf_op jit(solution)/shard_map/all_gather | solution.py:14
  22.9 0.3 fusion.1
  23.2 0.5 add_rsqrt_fusion
  23.7 171.5 %all-gather.4.cloned.1.call-done = bf16[3584,5120]{1,0:T(8,128)(2,1)} async-done(((bf16[224,5120]{1,0:T(8,128)(2,1)}), bf16[3584,5120]{1,0:T(8,128)(2,1)}) %all-gather.4.cloned.1.call-update) | async-done | bytes 36700176 | tf_op jit(solution)/shard_map/all_gather | solution.py:22
  195.2 15.6 %fusion.9 = f32[128,5120]{1,0:T(8,128)S(1)} fusion(bf16[3584,5120]{1,0:T(8,128)(2,1)} %all-gather.4.cloned.1.call-done, bf16[128,3584]{1,0:T(8,128)(2,1)S(1)} %all_gather.12, f32[3584]{0:T(1024)S(1)} %convert_element_type.23, f32[128]{0:T(128)} %add_rsqrt_fusion), kind=kOutput, calls=%fused_computation.16 | convolution fusion | flops 4699455488 | bytes 40253952 | tf_op jit(solution)/shard_map/dot_general | solution.py:20
  210.8 168.9 %all-gather.6.cloned.1.call-done = bf16[3584,5120]{1,0:T(8,128)(2,1)} async-done(((bf16[224,5120]{1,0:T(8,128)(2,1)}), bf16[3584,5120]{1,0:T(8,128)(2,1)}) %all-gather.6.cloned.1.call-update) | async-done | bytes 36700176 | tf_op jit(solution)/shard_map/all_gather | solution.py:23
  379.7 18.0 %fusion = bf16[128,5120]{1,0:T(8,128)(2,1)} fusion(bf16[3584,5120]{1,0:T(8,128)(2,1)} %all-gather.6.cloned.1.call-done, f32[128,5120]{1,0:T(8,128)S(1)} %fusion.9, bf16[128,3584]{1,0:T(8,128)(2,1)S(1)} %all_gather.12, f32[3584]{0:T(1024)S(1)} %convert_element_type.23, f32[128]{0:T(128)} %add_rsqrt_fusion), kind=kOutput, calls=%fused_computation.2 | convolution fusion | flops 4703387648 | bytes 41564672 | tf_op jit(solution)/shard_map/dot_general | solution.py:20
  397.7 0.0 all-gather.8.cloned.1.call-update
  397.7 0.2 reduce-scatter.2.cloned.1.call-start
  397.9 6.5 %pad_maximum_fusion = bf16[3,224,5120]{2,1,0:T(8,128)(2,1)} fusion(bf16[2,224,5120]{2,1,0:T(8,128)(2,1)} %param.11, bf16[1,224,5120]{2,1,0:T(8,128)(2,1)} %bitcast.13), kind=kLoop, calls=%fused_computation | loop fusion | flops 3440640 | bytes 13762560 | tf_op jit(solution)/shard_map/concatenate | solution.py:25
  404.4 102.2 %all-gather.8.cloned.1.call-done = bf16[2048,5120]{1,0:T(8,128)(2,1)} async-done(((bf16[128,5120]{1,0:T(8,128)(2,1)}), bf16[2048,5120]{1,0:T(8,128)(2,1)}) %all-gather.8.cloned.1.call-update) | async-done | bytes 20971536 | tf_op jit(solution)/shard_map/all_gather | solution.py:30
  506.6 21.8 %convolution_convert_fusion = bf16[2048,672]{0,1:T(8,128)(2,1)} fusion(bf16[2048,5120]{1,0:T(8,128)(2,1)} %all-gather.8.cloned.1.call-done, bf16[672,5120]{1,0:T(8,128)(2,1)} %bitcast.12), kind=kOutput, calls=%fused_computation.3 | convolution fusion | flops 14094237696 | bytes 30605312 | tf_op jit(solution)/shard_map/dot_general | solution.py:29
  528.4 0.0 reduce-scatter.2.cloned.1.call-update
  528.4 39.3 %reduce-scatter.2.cloned.1.call-done = bf16[1024,672]{0,1:T(8,128)(2,1)} async-done(((bf16[2048,672]{0,1:T(8,128)(2,1)}), bf16[1024,672]{0,1:T(8,128)(2,1)}) %reduce-scatter.2.cloned.1.call-update) | async-done | bytes 1376272 | tf_op jit(solution)/shard_map/reduce_scatter | solution.py:35
  567.7 1.7 convert.1
  569.4 0.2 fusion.4
  569.6 0.8 fusion.7
  570.5 0.3 fusion.6
  570.8 33.6 %psum.7 = f32[1024]{0:T(1024)} all-reduce(f32[1024]{0:T(1024)S(1)} %broadcast_multiply_fusion), channel_id=1, replica_groups=mesh['fsdp'=16,'tp'=2] {'fsdp'}, use_global_device_ids=true, to_apply=%region_4.5 | all-reduce | flops 1024 | bytes 8192 | tf_op jit(solution)/shard_map/psum | solution.py:45
  (2 shorter events, 0.0 us)
Async XLA Ops:
  7.2 1.6 copy-start.1
  7.2 1.6 copy-start
  7.2 188.0 %all-gather.4.cloned.1.call-start = ((), (), s32[]{:S(2)}) async-start(), calls=%async_computation.1 | async-start | bytes 38993920 | tf_op jit(solution)/shard_map/all_gather | solution.py:22
  7.9 371.8 %all-gather.6.cloned.1.call-start = ((), (), s32[]{:S(2)}) async-start(), calls=%async_computation.2 | async-start | bytes 38993920 | tf_op jit(solution)/shard_map/all_gather | solution.py:23
  8.7 497.9 %all-gather.8.cloned.1.call-start = ((), (), s32[]{:S(2)}) async-start(), calls=%async_computation.3 | async-start | bytes 22282240 | tf_op jit(solution)/shard_map/all_gather | solution.py:30
  397.7 170.0 %reduce-scatter.2.cloned.1.call-start = ((), (), s32[]{:S(2)}) async-start(), calls=%async_computation.4 | async-start | bytes 4128768 | tf_op jit(solution)/shard_map/reduce_scatter | solution.py:35
Sparse Core Ops, SparseCore 0:
  9.6 185.5 all-gather.3
  196.8 182.8 all-gather.5
  397.8 108.7 all-gather.7
  528.6 39.0 reduce-scatter.1
where the time goes:
time: 611 us
  waiting for transfers between devices  483 us (79%)
  matrix products  55.4 us (9%)
  blocking collectives  47.7 us (8%)
  between operations  13.8 us (2%)
  other arithmetic  9.52 us (2%)
    all_gather x1, waiting for transfers between devices, on_device(): gate_sum = add_rows(lax.all_gather(gate_weight, 'fsdp', axis=0, tiled=True))  171 us
    all_gather x1, waiting for transfers between devices, on_device(): up_sum = add_rows(lax.all_gather(up_weight, 'fsdp', axis=0, tiled=True))  169 us
    all_gather x1, waiting for transfers between devices, on_device(): lax.all_gather(hidden, 'fsdp', axis=0, tiled=True)  102 us
    reduce_scatter x1, waiting for transfers between devices, on_device(): lax.psum_scatter(partial_terms.astype(jnp.bfloat16), 'tp', scatter_dimens...  39.3 us
    dot_general x2, matrix products, add_rows(): return jnp.dot(normed, shard_rows, preferred_element_type=jnp.float32)  33.6 us
    psum x1, blocking collectives, on_device(): token_curv = lax.psum(local_curv, 'fsdp')  33.6 us
    dot_general x1, matrix products, on_device(): lax.dot_general(lax.all_gather(hidden, 'fsdp', axis=0, tiled=True), flat_...  21.8 us
    all_gather x1, blocking collectives, on_device(): features = lax.all_gather(tokens, 'tp', axis=1, tiled=True)  14.2 us
  transfers between devices with their start and end apart: 4, of which 4 were waited for; matrix products, arithmetic and copies ran while one was open for 4% of the time, Pallas kernels for 0%

commit v1 on v0

v1 whole, which is shorter than its diff:
```python
import jax
import jax.numpy as jnp
from jax import lax
from jax.experimental import pallas as pl
from jax.experimental.pallas import tpu as pltpu
from jax.sharding import PartitionSpec as P

D = 3584
PROBES = 2
MESH = pl.DeviceIdType.MESH
ANY = pl.BlockSpec(memory_space=pl.ANY)


epsilon = 1e-06


def remote(src, dst, send, recv, device):
    return pltpu.make_async_remote_copy(
        src_ref=src,
        dst_ref=dst,
        send_sem=send,
        recv_sem=recv,
        device_id=device,
        device_id_type=MESH,
    )


def exchange_kernel(chips, t_ref, g_ref, u_ref, to, go, uo, bounce, t_bounce, w_send, w_recv, c_send, c_recv, t_send, t_recv, local_sem):
    me = lax.axis_index("fsdp")
    tp = lax.axis_index("tp")
    chip, core = me // 2, me % 2
    outer, inner = chip // 2, chip % 2
    outers = chips // 2
    rows, width = go.shape[2], go.shape[3]
    t_rows, t_cols = t_ref.shape
    partner = {"fsdp": chip * 2 + 1 - core}
    across = {"tp": 1 - tp}

    barrier = pltpu.get_barrier_semaphore()
    for d in range(1, chips):
        pl.semaphore_signal(barrier, inc=1, device_id={"fsdp": ((chip + d) % chips) * 2 + core}, device_id_type=MESH)
    pl.semaphore_signal(barrier, inc=1, device_id=partner, device_id_type=MESH)
    pl.semaphore_signal(barrier, inc=1, device_id=across, device_id_type=MESH)
    pl.semaphore_wait(barrier, chips + 1)

    def token_slot(half, owner):
        return to.at[pl.ds(pl.multiple_of(owner * t_rows, t_rows), t_rows), pl.ds(pl.multiple_of(half * t_cols, 128), t_cols)]

    def token_copy(src, half, owner, way, device):
        return remote(src, token_slot(half, owner), t_send.at[way, owner], t_recv.at[half, owner], device)

    down = {"fsdp": (chip - 2) * 2 + core}
    up = {"fsdp": (chip + 2) * 2 + core}
    side = {"fsdp": (outer * 2 + 1 - inner) * 2 + core}

    def pass_on(src, owner, first):
        if first in (0, 1):
            @pl.when(outer > 0)
            def _():
                token_copy(src, tp, owner, 0, down).start()
        if first in (0, 2):
            @pl.when(outer < outers - 1)
            def _():
                token_copy(src, tp, owner, 1, up).start()
        token_copy(src, tp, owner, 2, side).start()
        token_copy(src, tp, owner, 3, across).start()

    pass_on(t_ref, chip, 0)
    weights = ((g_ref, go), (u_ref, uo))
    order = sorted(range(1, chips), key=lambda d: -min(d // 2, (chips - d) // 2))
    sends = [(a, d) for a in range(2) for d in order]

    def weight_send(a, d):
        src, dst = weights[a]
        peer = (chip + d) % chips
        return remote(
            src.at[:, pl.ds(pl.multiple_of(peer * width, 128), width)],
            dst.at[chip, core],
            w_send.at[a, d],
            w_recv.at[a, chip],
            {"fsdp": peer * 2 + core},
        )

    batch = -(-len(sends) // outers)
    batches = [sends[i * batch : (i + 1) * batch] for i in range(outers)]
    for a, d in batches[0]:
        weight_send(a, d).start()

    def own(a):
        return weights[a][0].at[:, pl.ds(pl.multiple_of(chip * width, 128), width)]

    def own_out(a):
        return remote(own(a), weights[a][1].at[chip, core], c_send.at[a, chip], c_recv.at[a, chip], partner)

    for a in range(2):
        own_out(a).start()
        pltpu.make_async_copy(own(a), bounce.at[a], local_sem.at[a]).start()
    pltpu.make_async_copy(t_ref, t_bounce, local_sem.at[2]).start()
    for a in range(2):
        pltpu.make_async_copy(own(a), bounce.at[a], local_sem.at[a]).wait()
        pltpu.make_async_copy(bounce.at[a], weights[a][1].at[chip, core], local_sem.at[a]).start()
    pltpu.make_async_copy(t_ref, t_bounce, local_sem.at[2]).wait()
    pltpu.make_async_copy(t_bounce, token_slot(tp, chip), local_sem.at[2]).start()

    def token_wait(half, owner):
        slot = token_slot(half, owner)
        remote(slot, slot, t_send.at[3, owner], t_recv.at[half, owner], across).wait_recv()

    for r in range(1, outers):
        @pl.when(outer - r >= 0)
        def _():
            owner = chip - 2 * r
            token_wait(tp, owner)
            pass_on(token_slot(tp, owner), owner, 2)

        @pl.when(outer + r < outers)
        def _():
            owner = chip + 2 * r
            token_wait(tp, owner)
            pass_on(token_slot(tp, owner), owner, 1)

        for a, d in batches[r]:
            weight_send(a, d).start()

    def side_owner(z):
        return z * 2 + 1 - inner

    def weight_wait_forward(a, d):
        s = (chip + chips - d) % chips
        block = weights[a][1].at[s, core]
        remote(block, block, w_send.at[a, d], w_recv.at[a, s], partner).wait_recv()
        remote(block, block, c_send.at[a, s], c_recv.at[a, s], partner).start()

    for a, d in batches[0]:
        weight_wait_forward(a, d)
    for z in range(outers):
        owner = side_owner(z)
        token_wait(tp, owner)
        slot = token_slot(tp, owner)
        token_copy(slot, tp, owner, 3, across).start()
    for group in batches[1:]:
        for a, d in group:
            weight_wait_forward(a, d)
    for s in range(chips):
        token_wait(1 - tp, s)
        for a in range(2):
            block = weights[a][1].at[s, 1 - core]
            remote(block, block, c_send.at[a, s], c_recv.at[a, s], partner).wait_recv()

    def sent(owner, way):
        slot = token_slot(tp, owner)
        remote(slot, slot, t_send.at[way, owner], t_recv.at[tp, owner], across).wait_send()

    for a, d in sends:
        weight_send(a, d).wait_send()
    for s in range(chips):
        for a in range(2):
            block = weights[a][1].at[s, core]
            remote(block, block, c_send.at[a, s], c_recv.at[a, s], partner).wait_send()
        sent(s, 3)
    for r in range(outers):
        @pl.when(outer - r >= 0)
        def _():
            owner = chip - 2 * r
            sent(owner, 2)

            @pl.when(outer < outers - 1)
            def _():
                sent(owner, 1)

        @pl.when(outer + r < outers)
        def _():
            owner = chip + 2 * r
            if r > 0:
                sent(owner, 2)

            @pl.when(outer > 0)
            def _():
                sent(owner, 0)
    for a in range(2):
        pltpu.make_async_copy(bounce.at[a], weights[a][1].at[chip, core], local_sem.at[a]).wait()
    pltpu.make_async_copy(t_bounce, token_slot(tp, chip), local_sem.at[2]).wait()


def exchange(tokens, gate_weight, up_weight, chips):
    rows, columns = gate_weight.shape
    width = columns // chips
    t_rows, t_cols = tokens.shape
    weight = jax.ShapeDtypeStruct((chips, 2, rows, width), gate_weight.dtype)
    pieces = pltpu.SemaphoreType.DMA((2, chips))
    t, g, u = pl.pallas_call(
        lambda *refs: exchange_kernel(chips, *refs),
        out_shape=(jax.ShapeDtypeStruct((chips * t_rows, 2 * t_cols), tokens.dtype), weight, weight),
        in_specs=[ANY] * 3,
        out_specs=[ANY] * 3,
        scratch_shapes=[
            pltpu.VMEM((2, rows, width), gate_weight.dtype),
            pltpu.VMEM((t_rows, t_cols), tokens.dtype),
            pieces,
            pieces,
            pieces,
            pieces,
            pltpu.SemaphoreType.DMA((4, chips)),
            pieces,
            pltpu.SemaphoreType.DMA((3,)),
        ],
        compiler_params=pltpu.CompilerParams(collective_id=1, has_side_effects=True),
        name="exchange",
    )(tokens, gate_weight, up_weight)
    return t, g.reshape(-1, width), u.reshape(-1, width)


def norm(features, norm_gain):
    widened = features.astype(jnp.float32)
    inverse_rms = lax.rsqrt(jnp.mean(widened * widened, axis=1, keepdims=True) + epsilon)
    return (widened * inverse_rms * norm_gain.astype(jnp.float32)).astype(jnp.bfloat16)


def dot(a, b):
    return jnp.dot(a, b, preferred_element_type=jnp.float32)


def project(hidden_all, down_weight, probes):
    stacked = jnp.concatenate([down_weight[None], probes], axis=0)
    count = stacked.shape[0]
    col_width = stacked.shape[1]
    flat_weights = stacked.reshape(count * col_width, stacked.shape[2])
    partial_terms = lax.dot_general(
        hidden_all,
        flat_weights,
        (((1,), (1,)), ((), ())),
        preferred_element_type=jnp.float32,
    )
    summed = lax.psum_scatter(
        partial_terms.astype(jnp.bfloat16), "tp", scatter_dimension=0, tiled=True
    ).astype(jnp.float32)
    summed_parts = summed.reshape(summed.shape[0], count, col_width)
    primal = summed_parts[:, 0, :]
    tangents = summed_parts[:, 1:, :]
    squashed = jax.nn.sigmoid(primal)
    slope = squashed * (1.0 - squashed)
    tangent_sq = jnp.sum(tangents * tangents, axis=1)
    local_curv = jnp.sum(slope * tangent_sq, axis=1) / (PROBES * D)
    token_curv = lax.psum(local_curv, "fsdp")
    return (primal.astype(jnp.bfloat16), token_curv)


def gathered_weights(tokens, norm_gain, gate_weight, up_weight, down_weight, probes):
    normed = norm(lax.all_gather(tokens, "tp", axis=1, tiled=True), norm_gain)
    gate_sum = dot(normed, lax.all_gather(gate_weight, "fsdp", axis=0, tiled=True))
    up_sum = dot(normed, lax.all_gather(up_weight, "fsdp", axis=0, tiled=True))
    hidden = (jax.nn.silu(gate_sum) * up_sum).astype(jnp.bfloat16)
    return project(lax.all_gather(hidden, "fsdp", axis=0, tiled=True), down_weight, probes)


def moved_weights(tokens, norm_gain, gate_weight, up_weight, down_weight, probes):
    chips = lax.axis_size("fsdp") // 2
    features, gate, up = exchange(tokens, gate_weight, up_weight, chips)
    normed = norm(features, norm_gain)
    hidden = (jax.nn.silu(dot(normed, gate)) * dot(normed, up)).astype(jnp.bfloat16)
    blocks = lax.all_gather(hidden, "fsdp", axis=0)
    t_rows, width = tokens.shape[0], hidden.shape[1]
    blocks = blocks.reshape(chips, 2, chips, t_rows, width)
    hidden_all = blocks.transpose(2, 1, 3, 0, 4).reshape(2 * chips * t_rows, chips * width)
    return project(hidden_all, down_weight, probes)


def solution(mesh):
    def on_device(tokens, norm_gain, gate_weight, up_weight, down_weight, probes):
        chips = mesh.shape["fsdp"] // 2
        fits = mesh.shape["tp"] == 2 and chips % 2 == 0 and gate_weight.shape[1] % (128 * chips) == 0 and tokens.shape[1] % 128 == 0
        form = moved_weights if fits else gathered_weights
        return form(tokens, norm_gain, gate_weight, up_weight, down_weight, probes)

    return jax.shard_map(
        on_device,
        mesh=mesh,
        in_specs=(
            P("fsdp", "tp"),
            P(),
            P("fsdp", "tp"),
            P("fsdp", "tp"),
            P("fsdp", "tp"),
            P(None, "fsdp", "tp"),
        ),
        out_specs=(P("tp", "fsdp"), P("tp")),
        check_vma=False,
    )
```

time: 611 us -> 451 us (0.74)
  waiting for transfers between devices: 483 us -> 175 us
  Pallas kernels: 0 us -> 149 us
  local copies, waits for them, and re-layouts: 0.84 us -> 30.6 us
  matrix products: 55.4 us -> 35.7 us
  blocking collectives: 47.7 us -> 33.6 us
    all_gather x3 -> x1, waiting for transfers between devices: 443 us -> 135 us  [moved_weights(): blocks = lax.all_gather(hidden, 'fsdp', axis=0)]
    pallas_call x0 -> x1, Pallas kernels: none -> 149 us  [exchange(): pl.pallas_call(lambda *refs: exchange_kernel(chips, *refs), out_shape=(ja...]
    reshape x0 -> x1, local copies, waits for them, and re-layouts: none -> 20 us  [moved_weights(): blocks = blocks.reshape(chips, 2, chips, t_rows, width)]
    dot_general x3, matrix products: 55.4 us -> 35.7 us  [the longest x1 20.2 us: project(): lax.dot_general(hidden_all, flat_weights, (((1,), (1,)), ((), ())), prefe...]
    all_gather x1 -> x0, blocking collectives: 14.2 us -> none  [on_device(): features = lax.all_gather(tokens, 'tp', axis=1, tiled=True)]
    unnamed x4 -> x15, local copies, waits for them, and re-layouts: 0.01 us -> 9.76 us
  transfers between devices with their start and end apart: 4 -> 2, of which waited for: 4 -> 2; matrix products, arithmetic and copies ran while one was open for 4% -> 1% of each run, Pallas kernels for 0% -> 0%
where the time goes in v1:
time: 451 us
  waiting for transfers between devices  175 us (39%)
  Pallas kernels  149 us (33%)
  matrix products  35.7 us (8%)
  blocking collectives  33.6 us (7%)
  local copies, waits for them, and re-layouts  30.6 us (7%)
  between operations  14.2 us (3%)
  other arithmetic  12.7 us (3%)
    pallas_call x1, Pallas kernels, exchange(): pl.pallas_call(lambda *refs: exchange_kernel(chips, *refs), out_shape=(ja...  149 us
    all_gather x1, waiting for transfers between devices, moved_weights(): blocks = lax.all_gather(hidden, 'fsdp', axis=0)  135 us
    reduce_scatter x1, waiting for transfers between devices, project(): lax.psum_scatter(partial_terms.astype(jnp.bfloat16), 'tp', scatter_dimens...  39.3 us
    psum x1, blocking collectives, project(): token_curv = lax.psum(local_curv, 'fsdp')  33.6 us
    dot_general x1, matrix products, project(): lax.dot_general(hidden_all, flat_weights, (((1,), (1,)), ((), ())), prefe...  20.2 us
    reshape x1, local copies, waits for them, and re-layouts, moved_weights(): blocks = blocks.reshape(chips, 2, chips, t_rows, width)  20 us
    dot_general x2, matrix products, dot(): return jnp.dot(a, b, preferred_element_type=jnp.float32)  15.5 us
    unnamed x15, local copies, waits for them, and re-layouts  9.76 us
  transfers between devices with their start and end apart: 2, of which 2 were waited for; matrix products, arithmetic and copies ran while one was open for 1% of the time, Pallas kernels for 0%

profile of v1, /device:TPU:0, one launch (start us, length us, event | category | flops | bytes accessed | tf_op | source)
XLA Modules:
  0.0 451.1 jit_solution(5938483888420550121)
XLA Ops:
  7.2 0.0 copy-start.2
  7.2 0.0 all-gather.3.cloned.1.call-start
  7.2 149.5 %exchange.1 = (bf16[1024,3584]{1,0:T(8,128)(2,1)}, bf16[8,2,224,640]{3,2,1,0:T(8,128)(2,1)}, bf16[8,2,224,640]{3,2,1,0:T(8,128)(2,1)}) custom-call(bf16[128,1792]{1,0:T(8,128)(2,1)} %refs_0_.1, bf16[224,5120]{1,0:T(8,128)(2,1)} %refs_1_.1, bf16[224,5120]{1,0:T(8,128)(2,1)} %refs_2_.1), custom_call_target="tpu_custom_call" | custom-call | tf_op jit(solution)/shard_map/exchange/pallas_call | solution.py:191
  156.7 0.0 copy-start
  156.7 0.0 slice-start.2
  156.7 4.7 %fusion = f32[1024]{0:T(1024)S(1)} fusion(bf16[1024,3584]{1,0:T(8,128)(2,1)} %get-tuple-element.5), kind=kLoop, calls=%fused_computation.2 | loop fusion | flops 11009024 | bytes 7344128 | tf_op jit(solution)/shard_map/reduce_sum | solution.py:215
  161.5 0.0 copy-done.2
  161.5 0.4 copy-done
  161.9 0.0 slice-start.3
  161.9 8.3 %fusion.3 = f32[1024,640]{1,0:T(8,128)S(1)} fusion(bf16[3584,640]{1,0:T(8,128)(2,1)} %bitcast.30, bf16[1024,3584]{1,0:T(8,128)(2,1)S(1)} %copy-done, f32[3584]{0:T(1024)S(1)} %convert_element_type.23, f32[1024]{0:T(1024)S(1)} %add_rsqrt_fusion), kind=kOutput, calls=%fused_computation.8 | convolution fusion | flops 4712300544 | bytes 14567424 | tf_op jit(solution)/shard_map/dot_general | solution.py:220
  170.2 0.0 slice-done.2
  170.2 0.0 slice-done.3
  170.3 0.0 copy-start.1
  170.3 7.1 %multiply_convert_fusion = bf16[1024,640]{1,0:T(8,128)(2,1)} fusion(f32[1024,640]{1,0:T(8,128)S(1)} %fusion.3, bf16[3584,640]{1,0:T(8,128)(2,1)S(1)} %bitcast.29, bf16[1024,3584]{1,0:T(8,128)(2,1)S(1)} %copy-done, f32[3584]{0:T(1024)S(1)} %convert_element_type.23, f32[1024]{0:T(1024)S(1)} %add_rsqrt_fusion), kind=kOutput, calls=%fused_computation.7 | convolution fusion | flops 4716232704 | bytes 15878144 | tf_op jit(solution)/shard_map/dot_general | solution.py:220
  177.4 0.0 all-gather.3.cloned.1.call-update
  177.4 0.2 reduce-scatter.2.cloned.1.call-start
  177.7 0.0 copy-done.1
  177.7 5.8 %pad_maximum_fusion = bf16[3,224,5120]{2,1,0:T(8,128)(2,1)} fusion(bf16[2,224,5120]{2,1,0:T(8,128)(2,1)} %param.11, bf16[1,224,5120]{2,1,0:T(8,128)(2,1)S(1)} %bitcast.25), kind=kLoop, calls=%fused_computation.5 | loop fusion | flops 3440640 | bytes 13762560 | tf_op jit(solution)/shard_map/concatenate | solution.py:224
  183.4 135.3 %all-gather.3.cloned.1.call-done = bf16[16384,640]{1,0:T(8,128)(2,1)} async-done(((bf16[1024,640]{1,0:T(8,128)(2,1)}), bf16[16384,640]{1,0:T(8,128)(2,1)}) %all-gather.3.cloned.1.call-update) | async-done | bytes 20971536 | tf_op jit(solution)/shard_map/all_gather | solution.py:261
  318.7 0.0 slice-start
  318.7 20.0 %copy.8 = bf16[8,2,8,128,640]{4,0,3,1,2:T(8,128)(2,1)S(1)} copy(bf16[8,2,8,128,640]{4,3,2,1,0:T(8,128)(2,1)} %bitcast.20) | data formatting | bytes 41943040 | tf_op jit(solution)/shard_map/reshape | solution.py:263
  338.7 0.0 slice-start.1
  338.7 9.3 %copy.9 = bf16[256,8,8,640]{3,1,2,0:T(8,128)(2,1)} copy(bf16[256,8,8,640]{3,2,1,0:T(8,128)(2,1)S(1)} %bitcast.19) | data formatting | bytes 41943040
  348.1 0.0 slice-done
  348.1 0.0 slice-done.1
  348.1 20.2 %convolution_convert_fusion = bf16[2048,672]{0,1:T(8,128)(2,1)} fusion(bf16[2048,5120]{1,0:T(8,128)(2,1)} %bitcast.21, bf16[672,5120]{1,0:T(8,128)(2,1)S(1)} %bitcast.24), kind=kOutput, calls=%fused_computation.6 | convolution fusion | flops 14094237696 | bytes 30605312 | tf_op jit(solution)/shard_map/dot_general | solution.py:228
  368.3 0.0 reduce-scatter.2.cloned.1.call-update
  368.3 39.3 %reduce-scatter.2.cloned.1.call-done = bf16[1024,672]{0,1:T(8,128)(2,1)} async-done(((bf16[2048,672]{0,1:T(8,128)(2,1)}), bf16[1024,672]{0,1:T(8,128)(2,1)}) %reduce-scatter.2.cloned.1.call-update) | async-done | bytes 1376272 | tf_op jit(solution)/shard_map/reduce_scatter | solution.py:234
  407.5 1.7 convert.1
  409.2 0.2 fusion.7
  409.5 0.8 fusion.12
  410.3 0.3 fusion.11
  410.6 33.6 %psum.7 = f32[1024]{0:T(1024)} all-reduce(f32[1024]{0:T(1024)S(1)} %broadcast_multiply_fusion), channel_id=1, replica_groups=mesh['fsdp'=16,'tp'=2] {'fsdp'}, use_global_device_ids=true, to_apply=%region_4.5 | all-reduce | flops 1024 | bytes 8192 | tf_op jit(solution)/shard_map/psum | solution.py:244
  (5 shorter events, 0.0 us)
Async XLA Ops:
  7.2 154.3 %copy-start.2 = (bf16[3584]{0:T(1024)(128)(2,1)S(1)}, bf16[3584]{0:T(1024)(128)(2,1)}, u32[]{:S(2)}) copy-start(bf16[3584]{0:T(1024)(128)(2,1)} %param.7) | copy-start | bytes 21508
  7.2 311.6 %all-gather.3.cloned.1.call-start = ((), (), s32[]{:S(2)}) async-start(), calls=%async_computation.2 | async-start | bytes 22282240 | tf_op jit(solution)/shard_map/all_gather | solution.py:261
  156.7 5.2 %copy-start = (bf16[1024,3584]{1,0:T(8,128)(2,1)S(1)}, bf16[1024,3584]{1,0:T(8,128)(2,1)}, u32[]{:S(2)}) copy-start(bf16[1024,3584]{1,0:T(8,128)(2,1)} %get-tuple-element.5) | copy-start | bytes 22020100
  156.7 13.5 %slice-start.2 = ((s8[4587520]{0:T(1024)(128)(4,1)}), s8[393216]{0:T(1024)(128)(4,1)S(1)}, s32[]{:S(2)}) async-start(s8[4587520]{0:T(1024)(128)(4,1)} %bitcast.27), calls=%async_computation.5 | async-start | bytes 786432
  161.9 8.4 %slice-start.3 = ((s8[4587520]{0:T(1024)(128)(4,1)}), s8[4194304]{0:T(1024)(128)(4,1)S(1)}, s32[]{:S(2)}) async-start(s8[4587520]{0:T(1024)(128)(4,1)} %bitcast.27), calls=%async_computation.6 | async-start | bytes 8388608
  170.3 7.4 %copy-start.1 = (bf16[224,5120]{1,0:T(8,128)(2,1)S(1)}, bf16[224,5120]{1,0:T(8,128)(2,1)}, u32[]{:S(2)}) copy-start(bf16[224,5120]{1,0:T(8,128)(2,1)} %param.10) | copy-start | bytes 6881284
  177.4 230.1 %reduce-scatter.2.cloned.1.call-start = ((), (), s32[]{:S(2)}) async-start(), calls=%async_computation.1 | async-start | bytes 4128768 | tf_op jit(solution)/shard_map/reduce_scatter | solution.py:234
  318.7 29.3 %slice-start = ((s8[6881280]{0:T(1024)(128)(4,1)}), s8[4194304]{0:T(1024)(128)(4,1)S(1)}, s32[]{:S(2)}) async-start(s8[6881280]{0:T(1024)(128)(4,1)} %bitcast.22), calls=%async_computation.3 | async-start | bytes 8388608
  338.7 9.4 %slice-start.1 = ((s8[6881280]{0:T(1024)(128)(4,1)}), s8[2686976]{0:T(1024)(128)(4,1)S(1)}, s32[]{:S(2)}) async-start(s8[6881280]{0:T(1024)(128)(4,1)} %bitcast.22), calls=%async_computation.4 | async-start | bytes 5373952
Sparse Core Ops, SparseCore 0:
  177.5 141.1 all-gather.2
  368.4 39.0 reduce-scatter.1
